TPU v7x, 32 devices: a whole 2x2x4 slice. The times are simulated.
32 devices in a mesh: ctx: 16 (over z, y, x), fsdp: 2 (over core).
Axes of the slice: x: 2, y: 2, z: 4, core: 2. Of those that a mesh axis runs over, the one named last changes fastest.
Arguments:
- tokens: bfloat16 [4, 2048, 576], P('fsdp', 'ctx'), may hold values from -6 to 6
- positions: int32 [4, 2048], P('fsdp', 'ctx'), may hold values from 0 to 2047, as said below
- norm_attn: bfloat16 [2, 576], P(None, 'fsdp'), may hold values from 0.5 to 1.5
- w_query: bfloat16 [2, 576, 576], P(None, 'fsdp'), may hold values from -0.25 to 0.25
- w_key: bfloat16 [2, 576, 192], P(None, 'fsdp'), may hold values from -0.25 to 0.25
- w_value: bfloat16 [2, 576, 192], P(None, 'fsdp'), may hold values from -0.25 to 0.25
- w_out: bfloat16 [2, 576, 576], P(None, 'fsdp'), may hold values from -2 to 2
- norm_ffn: bfloat16 [2, 576], P(None, 'fsdp'), may hold values from 0.5 to 1.5
- w_gate: bfloat16 [2, 576, 1536], P(None, 'fsdp'), may hold values from -0.25 to 0.25
- w_up: bfloat16 [2, 576, 1536], P(None, 'fsdp'), may hold values from -0.25 to 0.25
- w_down: bfloat16 [2, 1536, 576], P(None, 'fsdp'), may hold values from -0.15625 to 0.15625
- cotangent: bfloat16 [4, 2048, 576], P('fsdp', 'ctx'), may hold values from -6 to 6
Outputs:
- output: bfloat16 [4, 2048, 576], P('fsdp', 'ctx')
- grad_tokens: float32 [4, 2048, 576], P('fsdp', 'ctx')
- grad_norm_attn: float32 [2, 576], P(None, 'fsdp')
- grad_query: float32 [2, 576, 576], P(None, 'fsdp')
- grad_key: float32 [2, 576, 192], P(None, 'fsdp')
- grad_value: float32 [2, 576, 192], P(None, 'fsdp')
- grad_out: float32 [2, 576, 576], P(None, 'fsdp')
- grad_norm_ffn: float32 [2, 576], P(None, 'fsdp')
- grad_gate: float32 [2, 576, 1536], P(None, 'fsdp')
- grad_up: float32 [2, 576, 1536], P(None, 'fsdp')
- grad_down: float32 [2, 1536, 576], P(None, 'fsdp')
Inputs may be any that keep to these rules, and one draw needn't show every extreme that they name: For each sequence the 2048 positions are 0 .. 2047 once each; index c of ctx holds, in order, the two runs of 64 consecutive positions of blocks b and 31 - b, with b a permutation over the devices drawn per sequence.
All inputs are finite; a program needn't handle non-finite values.
Results may differ from a plain program's by a relative error of at most 0.02.
Values may be sent and summed in bfloat16 or wider, within the bound.
A program may use at most 320 MiB of HBM per device.

v0:
```python
import jax
import jax.numpy as jnp
from jax import lax
from jax.sharding import PartitionSpec as P

HEADS = 9
KV_HEADS = 3
HEAD = 64
EPS = 1e-05
ROPE_BASE = 100000.0


def rotate(tensor, positions_row, direction_sign):
    half_size = tensor.shape[-1] // 2
    frequency = jnp.exp(
        jnp.arange(half_size, dtype=jnp.float32) * (-jnp.log(ROPE_BASE) / half_size)
    )
    angles = positions_row.astype(jnp.float32)[..., None] * frequency
    cosine = jnp.cos(angles)[..., None, :]
    sine_part = direction_sign * jnp.sin(angles)[..., None, :]
    first_half = tensor[..., :half_size]
    second_half = tensor[..., half_size:]
    return jnp.concatenate(
        [
            first_half * cosine - second_half * sine_part,
            second_half * cosine + first_half * sine_part,
        ],
        axis=-1,
    )


def normalize(values, gain):
    return values * lax.rsqrt(jnp.mean(values * values, axis=-1, keepdims=True) + EPS) * gain


def normalize_back(values, gain, incoming):
    inverse = lax.rsqrt(jnp.mean(values * values, axis=-1, keepdims=True) + EPS)
    scaled = incoming * gain
    grad_values = inverse * scaled - values * (inverse * inverse * inverse) * jnp.mean(
        scaled * values, axis=-1, keepdims=True
    )
    grad_gain = jnp.sum(incoming * values * inverse, axis=(0, 1))
    return (grad_values, grad_gain)


def scores_of(queries, keys_all, query_places, key_places):
    raw_scores = jnp.einsum(
        "qhge,khe->hgqk", queries, keys_all, preferred_element_type=jnp.float32
    ) * queries.shape[-1] ** (-0.5)
    visible = key_places[None, :] <= query_places[:, None]
    return jnp.where(visible[None, None], raw_scores, -1e30)


def attend(operands):
    queries, keys_all, values_all, query_places, key_places = operands
    scores = scores_of(queries, keys_all, query_places, key_places)
    row_top = jnp.max(scores, axis=-1, keepdims=True)
    exponent = jnp.exp(scores - row_top)
    row_total = jnp.sum(exponent, axis=-1, keepdims=True)
    probabilities = (exponent / row_total).astype(jnp.bfloat16)
    mixed = jnp.einsum(
        "hgqk,khe->qhge", probabilities, values_all, preferred_element_type=jnp.float32
    )
    return (mixed, row_top + jnp.log(row_total))


def attend_back(operands):
    queries, keys_all, values_all, query_places, key_places, log_total, grad_mixed = operands
    score_scale = queries.shape[-1] ** (-0.5)
    scores = scores_of(queries, keys_all, query_places, key_places)
    probabilities = jnp.exp(scores - log_total)
    grad_probs = jnp.einsum(
        "qhge,khe->hgqk", grad_mixed, values_all, preferred_element_type=jnp.float32
    )
    grad_scores = (
        probabilities * (grad_probs - jnp.sum(probabilities * grad_probs, axis=-1, keepdims=True))
    ).astype(jnp.bfloat16)
    grad_queries = (
        jnp.einsum("hgqk,khe->qhge", grad_scores, keys_all, preferred_element_type=jnp.float32)
        * score_scale
    )
    grad_keys = (
        jnp.einsum("hgqk,qhge->khe", grad_scores, queries, preferred_element_type=jnp.float32)
        * score_scale
    )
    grad_values = jnp.einsum(
        "hgqk,qhge->khe",
        probabilities.astype(jnp.bfloat16),
        grad_mixed,
        preferred_element_type=jnp.float32,
    )
    return (grad_queries, grad_keys, grad_values)


def layer_forward(inputs, positions, places, weights):
    gain_attn, w_query, w_key, w_value, w_out, gain_ffn, w_gate, w_up, w_down = weights
    seq_count, row_count, model_width = inputs.shape
    normed = normalize(inputs, gain_attn).astype(jnp.bfloat16)
    query_pre = jnp.einsum("srd,de->sre", normed, w_query, preferred_element_type=jnp.float32)
    key_pre = jnp.einsum("srd,de->sre", normed, w_key, preferred_element_type=jnp.float32)
    value_pre = jnp.einsum("srd,de->sre", normed, w_value, preferred_element_type=jnp.float32)
    queries = rotate(query_pre.reshape(seq_count, row_count, HEADS, HEAD), positions, 1.0).astype(
        jnp.bfloat16
    )
    queries = queries.reshape(seq_count, row_count, KV_HEADS, HEADS // KV_HEADS, HEAD)
    keys_own = rotate(key_pre.reshape(seq_count, row_count, KV_HEADS, HEAD), positions, 1.0).astype(
        jnp.bfloat16
    )
    keys_own = keys_own.reshape(seq_count, row_count, KV_HEADS * HEAD)
    values_own = value_pre.astype(jnp.bfloat16)
    keys_all, values_all = (
        lax.all_gather(keys_own, "ctx", axis=1, tiled=True),
        lax.all_gather(values_own, "ctx", axis=1, tiled=True),
    )
    length = keys_all.shape[1]
    mixed, log_total = lax.map(
        attend,
        (
            queries,
            keys_all.reshape(seq_count, length, KV_HEADS, HEAD),
            values_all.reshape(seq_count, length, KV_HEADS, HEAD),
            positions,
            places,
        ),
    )
    mixed_low = mixed.reshape(seq_count, row_count, model_width).astype(jnp.bfloat16)
    middle = inputs + jnp.einsum(
        "srd,de->sre", mixed_low, w_out, preferred_element_type=jnp.float32
    )
    normed_ffn = normalize(middle, gain_ffn).astype(jnp.bfloat16)
    gate_pre = jnp.einsum("srd,df->srf", normed_ffn, w_gate, preferred_element_type=jnp.float32)
    up_pre = jnp.einsum("srd,df->srf", normed_ffn, w_up, preferred_element_type=jnp.float32)
    hidden = (jax.nn.silu(gate_pre) * up_pre).astype(jnp.bfloat16)
    result = middle + jnp.einsum("srf,fd->srd", hidden, w_down, preferred_element_type=jnp.float32)
    record = (
        inputs,
        normed,
        queries,
        keys_own,
        values_own,
        keys_all,
        values_all,
        log_total,
        mixed_low,
        middle,
        normed_ffn,
        gate_pre,
        up_pre,
        hidden,
    )
    return (result, record)


def layer_backward(gradient, record, weights, positions, places):
    gain_attn, w_query, w_key, w_value, w_out, gain_ffn, w_gate, w_up, w_down = weights
    (
        inputs,
        normed,
        queries,
        keys_own,
        values_own,
        kept_keys,
        kept_values,
        log_total,
        mixed_low,
        middle,
        normed_ffn,
        gate_pre,
        up_pre,
        hidden,
    ) = record
    seq_count, row_count, model_width = inputs.shape
    grad_low = gradient.astype(jnp.bfloat16)
    grad_wdown = jnp.einsum("srf,srd->fd", hidden, grad_low, preferred_element_type=jnp.float32)
    grad_hidden = jnp.einsum("srd,fd->srf", grad_low, w_down, preferred_element_type=jnp.float32)
    sigmoid_gate = jax.nn.sigmoid(gate_pre)
    grad_gate = (
        grad_hidden * up_pre * sigmoid_gate * (1.0 + gate_pre * (1.0 - sigmoid_gate))
    ).astype(jnp.bfloat16)
    grad_up = (grad_hidden * gate_pre * sigmoid_gate).astype(jnp.bfloat16)
    grad_wgate = jnp.einsum(
        "srd,srf->df", normed_ffn, grad_gate, preferred_element_type=jnp.float32
    )
    grad_wup = jnp.einsum("srd,srf->df", normed_ffn, grad_up, preferred_element_type=jnp.float32)
    grad_normed_ffn = jnp.einsum(
        "srf,df->srd", grad_gate, w_gate, preferred_element_type=jnp.float32
    ) + jnp.einsum("srf,df->srd", grad_up, w_up, preferred_element_type=jnp.float32)
    grad_middle_norm, grad_gain_ffn = normalize_back(middle, gain_ffn, grad_normed_ffn)
    grad_middle = gradient + grad_middle_norm
    branch_low = grad_middle.astype(jnp.bfloat16)
    grad_wout = jnp.einsum("srd,sre->de", mixed_low, branch_low, preferred_element_type=jnp.float32)
    grad_mixed = jnp.einsum(
        "sre,de->srd", branch_low, w_out, preferred_element_type=jnp.float32
    ).astype(jnp.bfloat16)
    grad_mixed = grad_mixed.reshape(seq_count, row_count, KV_HEADS, HEADS // KV_HEADS, HEAD)
    keys_all, values_all = (
        lax.all_gather(keys_own, "ctx", axis=1, tiled=True),
        lax.all_gather(values_own, "ctx", axis=1, tiled=True),
    )
    length = keys_all.shape[1]
    grad_queries, grad_keys_all, grad_values_all = lax.map(
        attend_back,
        (
            queries,
            keys_all.reshape(seq_count, length, KV_HEADS, HEAD),
            values_all.reshape(seq_count, length, KV_HEADS, HEAD),
            positions,
            places,
            log_total,
            grad_mixed,
        ),
    )
    grad_keys, grad_values = (
        lax.psum_scatter(
            grad_keys_all.reshape(seq_count, length, KV_HEADS * HEAD),
            "ctx",
            scatter_dimension=1,
            tiled=True,
        ),
        lax.psum_scatter(
            grad_values_all.reshape(seq_count, length, KV_HEADS * HEAD),
            "ctx",
            scatter_dimension=1,
            tiled=True,
        ),
    )
    grad_query_pre = (
        rotate(grad_queries.reshape(seq_count, row_count, HEADS, HEAD), positions, -1.0)
        .reshape(seq_count, row_count, model_width)
        .astype(jnp.bfloat16)
    )
    grad_key_pre = (
        rotate(grad_keys.reshape(seq_count, row_count, KV_HEADS, HEAD), positions, -1.0)
        .reshape(seq_count, row_count, KV_HEADS * HEAD)
        .astype(jnp.bfloat16)
    )
    grad_value_pre = grad_values.astype(jnp.bfloat16)
    grad_wquery = jnp.einsum(
        "srd,sre->de", normed, grad_query_pre, preferred_element_type=jnp.float32
    )
    grad_wkey = jnp.einsum("srd,sre->de", normed, grad_key_pre, preferred_element_type=jnp.float32)
    grad_wvalue = jnp.einsum(
        "srd,sre->de", normed, grad_value_pre, preferred_element_type=jnp.float32
    )
    grad_normed = jnp.einsum(
        "sre,de->srd", grad_query_pre, w_query, preferred_element_type=jnp.float32
    )
    grad_normed = grad_normed + jnp.einsum(
        "sre,de->srd", grad_key_pre, w_key, preferred_element_type=jnp.float32
    )
    grad_normed = grad_normed + jnp.einsum(
        "sre,de->srd", grad_value_pre, w_value, preferred_element_type=jnp.float32
    )
    grad_input_norm, grad_gain_attn = normalize_back(inputs, gain_attn, grad_normed)
    layer_grads = (
        grad_gain_attn,
        grad_wquery,
        grad_wkey,
        grad_wvalue,
        grad_wout,
        grad_gain_ffn,
        grad_wgate,
        grad_wup,
        grad_wdown,
    )
    return (grad_middle + grad_input_norm, layer_grads)


def body(
    tokens,
    positions,
    norm_attn,
    w_query,
    w_key,
    w_value,
    w_out,
    norm_ffn,
    w_gate,
    w_up,
    w_down,
    cotangent,
):
    layer_count = norm_attn.shape[0]
    places = lax.all_gather(positions, "ctx", axis=1, tiled=True)
    current = tokens.astype(jnp.float32)
    records = []
    gathered_weights = []
    for layer_index in range(layer_count):
        weights = (
            lax.all_gather(norm_attn[layer_index], "fsdp", axis=0, tiled=True),
            lax.all_gather(w_query[layer_index], "fsdp", axis=0, tiled=True),
            lax.all_gather(w_key[layer_index], "fsdp", axis=0, tiled=True),
            lax.all_gather(w_value[layer_index], "fsdp", axis=0, tiled=True),
            lax.all_gather(w_out[layer_index], "fsdp", axis=0, tiled=True),
            lax.all_gather(norm_ffn[layer_index], "fsdp", axis=0, tiled=True),
            lax.all_gather(w_gate[layer_index], "fsdp", axis=0, tiled=True),
            lax.all_gather(w_up[layer_index], "fsdp", axis=0, tiled=True),
            lax.all_gather(w_down[layer_index], "fsdp", axis=0, tiled=True),
        )
        current, record = layer_forward(current, positions, places, weights)
        records.append(record)
        gathered_weights.append(weights)
    output = current.astype(jnp.bfloat16)
    gradient = cotangent.astype(jnp.float32)
    collected = []
    for layer_index in reversed(range(layer_count)):
        weights = (
            lax.all_gather(norm_attn[layer_index], "fsdp", axis=0, tiled=True),
            lax.all_gather(w_query[layer_index], "fsdp", axis=0, tiled=True),
            lax.all_gather(w_key[layer_index], "fsdp", axis=0, tiled=True),
            lax.all_gather(w_value[layer_index], "fsdp", axis=0, tiled=True),
            lax.all_gather(w_out[layer_index], "fsdp", axis=0, tiled=True),
            lax.all_gather(norm_ffn[layer_index], "fsdp", axis=0, tiled=True),
            lax.all_gather(w_gate[layer_index], "fsdp", axis=0, tiled=True),
            lax.all_gather(w_up[layer_index], "fsdp", axis=0, tiled=True),
            lax.all_gather(w_down[layer_index], "fsdp", axis=0, tiled=True),
        )
        gradient, layer_grads = layer_backward(
            gradient, records[layer_index], weights, positions, places
        )
        shares = (
            lax.psum_scatter(
                layer_grads[0].astype(jnp.bfloat16), "fsdp", scatter_dimension=0, tiled=True
            ).astype(jnp.float32),
            lax.psum_scatter(
                layer_grads[1].astype(jnp.bfloat16), "fsdp", scatter_dimension=0, tiled=True
            ).astype(jnp.float32),
            lax.psum_scatter(
                layer_grads[2].astype(jnp.bfloat16), "fsdp", scatter_dimension=0, tiled=True
            ).astype(jnp.float32),
            lax.psum_scatter(
                layer_grads[3].astype(jnp.bfloat16), "fsdp", scatter_dimension=0, tiled=True
            ).astype(jnp.float32),
            lax.psum_scatter(
                layer_grads[4].astype(jnp.bfloat16), "fsdp", scatter_dimension=0, tiled=True
            ).astype(jnp.float32),
            lax.psum_scatter(
                layer_grads[5].astype(jnp.bfloat16), "fsdp", scatter_dimension=0, tiled=True
            ).astype(jnp.float32),
            lax.psum_scatter(
                layer_grads[6].astype(jnp.bfloat16), "fsdp", scatter_dimension=0, tiled=True
            ).astype(jnp.float32),
            lax.psum_scatter(
                layer_grads[7].astype(jnp.bfloat16), "fsdp", scatter_dimension=0, tiled=True
            ).astype(jnp.float32),
            lax.psum_scatter(
                layer_grads[8].astype(jnp.bfloat16), "fsdp", scatter_dimension=0, tiled=True
            ).astype(jnp.float32),
        )
        totals = lax.psum(
            (
                shares[0],
                shares[1],
                shares[2],
                shares[3],
                shares[4],
                shares[5],
                shares[6],
                shares[7],
                shares[8],
            ),
            "ctx",
        )
        collected.insert(0, totals)
    stacked = tuple(
        (jnp.stack([entry_totals[member] for entry_totals in collected]) for member in range(9))
    )
    return (
        output,
        gradient,
        stacked[0],
        stacked[1],
        stacked[2],
        stacked[3],
        stacked[4],
        stacked[5],
        stacked[6],
        stacked[7],
        stacked[8],
    )


def solution(mesh):
    in_specs = (
        P("fsdp", "ctx", None),
        P("fsdp", "ctx"),
        P(None, "fsdp"),
        P(None, "fsdp", None),
        P(None, "fsdp", None),
        P(None, "fsdp", None),
        P(None, "fsdp", None),
        P(None, "fsdp"),
        P(None, "fsdp", None),
        P(None, "fsdp", None),
        P(None, "fsdp", None),
        P("fsdp", "ctx", None),
    )
    out_specs = (
        P("fsdp", "ctx", None),
        P("fsdp", "ctx", None),
        P(None, "fsdp"),
        P(None, "fsdp", None),
        P(None, "fsdp", None),
        P(None, "fsdp", None),
        P(None, "fsdp", None),
        P(None, "fsdp"),
        P(None, "fsdp", None),
        P(None, "fsdp", None),
        P(None, "fsdp", None),
    )
    return jax.shard_map(body, mesh=mesh, in_specs=in_specs, out_specs=out_specs, check_vma=False)
```

profile of v0, /device:TPU:0, one launch (start us, length us, event | category | flops | bytes accessed | tf_op | source)
XLA Modules:
  0.0 1770.1 jit_solution(10200862059027686231)
XLA Ops:
  31.5 42.7 %all_gather.94 = s32[2,2048]{1,0:T(2,128)S(1)} all-gather(s32[2,128]{1,0:T(2,128)S(1)} %copy-done.116), channel_id=1, replica_groups=mesh['ctx'=16,'fsdp'=2] {'ctx'}, dimensions={1}, use_global_device_ids=true | all-gather | bytes 17408 | tf_op jit(solution)/shard_map/all_gather | solution.py:284
  86.0 50.3 %all-gather.31.cloned.1.call-done = bf16[2,2048,192]{1,2,0:T(8,128)(2,1)} async-done(((bf16[2,128,192]{1,2,0:T(8,128)(2,1)}), bf16[2,2048,192]{1,2,0:T(8,128)(2,1)}) %all-gather.31.cloned.1.call-update) | async-done | bytes 1572880 | tf_op jit(solution)/shard_map/all_gather | solution.py:112
  136.3 15.6 while.52
  164.0 8.7 all-gather.41.cloned.1.call-done
  191.8 55.6 %all-gather.33.cloned.1.call-done = bf16[2,2048,192]{1,2,0:T(8,128)(2,1)} async-done(((bf16[2,128,192]{1,2,0:T(8,128)(2,1)}), bf16[2,2048,192]{1,2,0:T(8,128)(2,1)}) %all-gather.33.cloned.1.call-update) | async-done | bytes 1572880 | tf_op jit(solution)/shard_map/all_gather | solution.py:113
  247.4 58.3 %all-gather.35.cloned.1.call-done = bf16[2,2048,192]{1,2,0:T(8,128)(2,1)} async-done(((bf16[2,128,192]{1,2,0:T(8,128)(2,1)}), bf16[2,2048,192]{1,2,0:T(8,128)(2,1)}) %all-gather.35.cloned.1.call-update) | async-done | bytes 1572880 | tf_op jit(solution)/shard_map/all_gather | solution.py:112
  305.7 15.6 while.53
  344.0 63.8 %while.54 = (s32[]{:T(128)}, f32[2,128,3,3,64]{1,4,3,2,0:T(8,128)}, f32[2,2048,3,64]{1,3,2,0:T(8,128)}, f32[2,2048,3,64]{1,3,2,0:T(8,128)}, bf16[2,2048,3,64]{1,...) while((s32[]{:T(128)}, f32[2,128,3,3,64]{1,4,3,2,0:T(8,128)}, ...), condition=%wide.region_15.16_spmd, body=%wide.region_13.15_spmd.sunk | while | flops 1546066816 | bytes 160072944 | solution.py:201
  346.0 5.8 fusion.325
  351.9 11.1 fusion.326
  367.1 5.3 fusion.328
  377.8 5.8 fusion.325
  383.7 11.1 fusion.326
  398.8 5.3 fusion.328
  421.1 120.8 %reduce-scatter.19.cloned.1.call-done = f32[2,128,192]{1,2,0:T(8,128)} async-done(((f32[2,2048,192]{1,2,0:T(8,128)}), f32[2,128,192]{1,2,0:T(8,128)}) %reduce-scatter.19.cloned.1.call-update) | async-done | bytes 196624 | tf_op jit(solution)/shard_map/reduce_scatter | solution.py:214
  544.5 134.7 %reduce-scatter.21.cloned.1.call-done = f32[2,128,192]{1,2,0:T(8,128)} async-done(((f32[2,2048,192]{1,2,0:T(8,128)}), f32[2,128,192]{1,2,0:T(8,128)}) %reduce-scatter.21.cloned.1.call-update) | async-done | bytes 196624 | tf_op jit(solution)/shard_map/reduce_scatter | solution.py:220
  696.9 65.5 %while.55 = (s32[]{:T(128)}, f32[2,128,3,3,64]{1,4,3,2,0:T(8,128)}, f32[2,2048,3,64]{1,3,2,0:T(8,128)}, f32[2,2048,3,64]{1,3,2,0:T(8,128)}, bf16[2,2048,3,64]{1,...) while((s32[]{:T(128)}, f32[2,128,3,3,64]{1,4,3,2,0:T(8,128)}, ...), condition=%wide.region_22.23_spmd, body=%wide.region_20.22_spmd.sunk | while | flops 1546066816 | bytes 160072944 | solution.py:201
  698.8 5.8 fusion.340
  704.8 11.8 fusion.341
  720.6 5.8 fusion.343
  731.9 5.8 fusion.340
  738.4 11.1 fusion.341
  753.5 5.3 fusion.343
  795.6 10.8 reduce-scatter.43.cloned.1.call-done
  809.0 137.1 %reduce-scatter.23.cloned.1.call-done = f32[2,128,192]{1,2,0:T(8,128)} async-done(((f32[2,2048,192]{1,2,0:T(8,128)}), f32[2,128,192]{1,2,0:T(8,128)}) %reduce-scatter.23.cloned.1.call-update) | async-done | bytes 196624 | tf_op jit(solution)/shard_map/reduce_scatter | solution.py:214
  948.2 8.3 reduce-scatter.47.cloned.1.call-done
  959.1 137.1 %reduce-scatter.25.cloned.1.call-done = f32[2,128,192]{1,2,0:T(8,128)} async-done(((f32[2,2048,192]{1,2,0:T(8,128)}), f32[2,128,192]{1,2,0:T(8,128)}) %reduce-scatter.25.cloned.1.call-update) | async-done | bytes 196624 | tf_op jit(solution)/shard_map/reduce_scatter | solution.py:220
  1098.2 8.3 reduce-scatter.51.cloned.1.call-done
  1109.0 9.2 reduce-scatter.31.cloned.1.call-done
  1119.9 10.1 reduce-scatter.35.cloned.1.call-done
  1140.7 45.2 %all-reduce.8 = (f32[1,288]{1,0:T(1,128)S(1)}, f32[1,288]{1,0:T(1,128)S(1)}, f32[1,288]{1,0:T(1,128)S(1)}, f32[1,288]{1,0:T(1,128)S(1)}) all-reduce(f32[1,288]{1,0:T(1,128)S(1)} %stack.82, f32[1,288]{1,0:T(1,128)S(1)} %stack.81, f32[1,288]{1,0:T(1,128)S(1)} %stack.97, ...), channel_id=1, replica_groups=mesh['ctx'=16,'fsdp'=2] {'ctx'}, use_global_device_ids=true, to_apply=%region_31.32 | all-reduce | flops 1152 | bytes 9216 | tf_op jit(solution)/shard_map/psum | solution.py:350
  1188.1 562.2 %all-reduce.14.cloned.1.call-done = (f32[1,288,576]{2,1,0:T(8,128)}, f32[1,288,576]{2,1,0:T(8,128)}, f32[1,288,192]{2,1,0:T(8,128)}, f32[1,288,192]{2,1,0:T(8,12...) async-done(((f32[1,288,576]{2,1,0:T(8,128)}, ...) | async-done | bytes 14155792 | tf_op jit(solution)/shard_map/psum | solution.py:350
  (533 shorter events, 262.7 us)
Async XLA Ops:
  7.2 78.8 %all-gather.29.cloned.1.call-start = ((), (), s32[]{:S(2)}) async-start(), calls=%async_computation.18 | async-start | bytes 1671168 | tf_op jit(solution)/shard_map/all_gather | solution.py:113
  19.0 117.3 %all-gather.31.cloned.1.call-start = ((), (), s32[]{:S(2)}) async-start(), calls=%async_computation.19 | async-start | bytes 1671168 | tf_op jit(solution)/shard_map/all_gather | solution.py:112
  23.9 167.8 %copy-start.58 = (f32[2,128,32]{1,2,0:T(8,128)}, f32[2,128,32]{1,2,0:T(8,128)S(1)}, u32[]{:S(2)}) copy-start(f32[2,128,32]{1,2,0:T(8,128)S(1)} %get-tuple-element.386) | copy-start | bytes 98308
  25.0 128.2 %all-gather.37.cloned.1.call-start = ((), (), s32[]{:S(2)}) async-start(), calls=%async_computation.40 | async-start | bytes 2654208 | tf_op jit(solution)/shard_map/all_gather | solution.py:296
  26.4 133.6 %all-gather.39.cloned.1.call-start = ((), (), s32[]{:S(2)}) async-start(), calls=%async_computation.41 | async-start | bytes 2654208 | tf_op jit(solution)/shard_map/all_gather | solution.py:297
  29.4 143.3 %all-gather.41.cloned.1.call-start = ((), (), s32[]{:S(2)}) async-start(), calls=%async_computation.42 | async-start | bytes 2654208 | tf_op jit(solution)/shard_map/all_gather | solution.py:298
  30.8 157.0 %all-gather.47.cloned.1.call-start = ((), (), s32[]{:S(2)}) async-start(), calls=%async_computation.45 | async-start | bytes 2654208 | tf_op jit(solution)/shard_map/all_gather | solution.py:298
  31.4 216.0 %all-gather.33.cloned.1.call-start = ((), (), s32[]{:S(2)}) async-start(), calls=%async_computation.20 | async-start | bytes 1671168 | tf_op jit(solution)/shard_map/all_gather | solution.py:113
  176.5 129.2 %all-gather.35.cloned.1.call-start = ((), (), s32[]{:S(2)}) async-start(), calls=%async_computation.21 | async-start | bytes 1671168 | tf_op jit(solution)/shard_map/all_gather | solution.py:112
  181.1 140.9 %all-gather.45.cloned.1.call-start = ((), (), s32[]{:S(2)}) async-start(), calls=%async_computation.44 | async-start | bytes 2654208 | tf_op jit(solution)/shard_map/all_gather | solution.py:297
  181.8 147.6 %all-gather.43.cloned.1.call-start = ((), (), s32[]{:S(2)}) async-start(), calls=%async_computation.43 | async-start | bytes 2654208 | tf_op jit(solution)/shard_map/all_gather | solution.py:296
  182.4 359.5 %reduce-scatter.19.cloned.1.call-start = ((), (), s32[]{:S(2)}) async-start(), calls=%async_computation.22 | async-start | bytes 3342336 | tf_op jit(solution)/shard_map/reduce_scatter | solution.py:214
  407.8 271.4 %reduce-scatter.21.cloned.1.call-start = ((), (), s32[]{:S(2)}) async-start(), calls=%async_computation.23 | async-start | bytes 3342336 | tf_op jit(solution)/shard_map/reduce_scatter | solution.py:220
  408.4 365.8 %reduce-scatter.29.cloned.1.call-start = ((), (), s32[]{:S(2)}) async-start(), calls=%async_computation.27 | async-start | bytes 1105920 | tf_op jit(solution)/shard_map/reduce_scatter | solution.py:325
  410.3 367.8 %reduce-scatter.41.cloned.1.call-start = ((), (), s32[]{:S(2)}) async-start(), calls=%async_computation.33 | async-start | bytes 1105920 | tf_op jit(solution)/shard_map/reduce_scatter | solution.py:334
  411.8 368.3 %reduce-scatter.53.cloned.1.call-start = ((), (), s32[]{:S(2)}) async-start(), calls=%async_computation.39 | async-start | bytes 2654208 | tf_op jit(solution)/shard_map/reduce_scatter | solution.py:346
  414.8 367.7 %reduce-scatter.45.cloned.1.call-start = ((), (), s32[]{:S(2)}) async-start(), calls=%async_computation.35 | async-start | bytes 2654208 | tf_op jit(solution)/shard_map/reduce_scatter | solution.py:340
  417.9 367.2 %reduce-scatter.49.cloned.1.call-start = ((), (), s32[]{:S(2)}) async-start(), calls=%async_computation.37 | async-start | bytes 2654208 | tf_op jit(solution)/shard_map/reduce_scatter | solution.py:343
  421.0 258.1 %copy-start.103 = (f32[576]{0:T(1024)S(1)}, f32[576]{0:T(1024)}, u32[]{:S(2)}) copy-start(f32[576]{0:T(1024)} %copy-done.102) | copy-start | bytes 6916
  421.1 258.1 %copy-start.109 = (f32[2,128]{1,0:T(2,128)S(1)}, f32[2,128]{1,0:T(2,128)}, u32[]{:S(2)}) copy-start(f32[2,128]{1,0:T(2,128)} %copy-done.108) | copy-start | bytes 3076
  421.1 366.6 %reduce-scatter.33.cloned.1.call-start = ((), (), s32[]{:S(2)}) async-start(), calls=%async_computation.29 | async-start | bytes 442368 | tf_op jit(solution)/shard_map/reduce_scatter | solution.py:328
  691.6 97.7 %reduce-scatter.37.cloned.1.call-start = ((), (), s32[]{:S(2)}) async-start(), calls=%async_computation.31 | async-start | bytes 442368 | tf_op jit(solution)/shard_map/reduce_scatter | solution.py:331
  764.4 26.6 %reduce-scatter.27.cloned.1.call-start = ((), (), s32[]{:S(2)}) async-start(), calls=%async_computation.26 | async-start | bytes 1105920 | tf_op jit(solution)/shard_map/reduce_scatter | solution.py:325
  767.0 26.7 %reduce-scatter.39.cloned.1.call-start = ((), (), s32[]{:S(2)}) async-start(), calls=%async_computation.32 | async-start | bytes 1105920 | tf_op jit(solution)/shard_map/reduce_scatter | solution.py:334
  768.4 38.0 %reduce-scatter.43.cloned.1.call-start = ((), (), s32[]{:S(2)}) async-start(), calls=%async_computation.34 | async-start | bytes 2654208 | tf_op jit(solution)/shard_map/reduce_scatter | solution.py:340
  770.3 175.8 %reduce-scatter.23.cloned.1.call-start = ((), (), s32[]{:S(2)}) async-start(), calls=%async_computation.24 | async-start | bytes 3342336 | tf_op jit(solution)/shard_map/reduce_scatter | solution.py:214
  771.0 185.4 %reduce-scatter.47.cloned.1.call-start = ((), (), s32[]{:S(2)}) async-start(), calls=%async_computation.36 | async-start | bytes 2654208 | tf_op jit(solution)/shard_map/reduce_scatter | solution.py:343
  773.4 322.8 %reduce-scatter.25.cloned.1.call-start = ((), (), s32[]{:S(2)}) async-start(), calls=%async_computation.25 | async-start | bytes 3342336 | tf_op jit(solution)/shard_map/reduce_scatter | solution.py:220
  774.1 332.3 %reduce-scatter.51.cloned.1.call-start = ((), (), s32[]{:S(2)}) async-start(), calls=%async_computation.38 | async-start | bytes 2654208 | tf_op jit(solution)/shard_map/reduce_scatter | solution.py:346
  778.0 340.2 %reduce-scatter.31.cloned.1.call-start = ((), (), s32[]{:S(2)}) async-start(), calls=%async_computation.28 | async-start | bytes 442368 | tf_op jit(solution)/shard_map/reduce_scatter | solution.py:328
  948.1 181.8 %reduce-scatter.35.cloned.1.call-start = ((), (), s32[]{:S(2)}) async-start(), calls=%async_computation.30 | async-start | bytes 442368 | tf_op jit(solution)/shard_map/reduce_scatter | solution.py:331
  1098.1 652.2 %all-reduce.14.cloned.1.call-start = ((), (), s32[]{:S(2)}) async-start(), calls=%async_computation.46 | async-start | bytes 29491200 | tf_op jit(solution)/shard_map/psum | solution.py:350
  (123 other events, 1760.9 us)
Sparse Core Ops, SparseCore 0:
  19.1 59.4 all-gather.28
  81.2 54.9 all-gather.30
  138.4 8.3 all-gather.36
  148.8 11.1 all-gather.38
  161.4 11.2 all-gather.40
  174.6 11.4 all-gather.46
  189.4 57.9 all-gather.32
  250.7 54.9 all-gather.34
  307.8 8.3 all-gather.44
  318.2 11.1 all-gather.42
  407.9 134.0 reduce-scatter.18
  547.4 131.7 reduce-scatter.20
  681.4 7.0 reduce-scatter.28
  690.7 9.1 reduce-scatter.40
  702.0 10.3 reduce-scatter.52
  715.1 10.5 reduce-scatter.44
  727.8 10.5 reduce-scatter.48
  741.1 9.0 reduce-scatter.32
  764.5 6.1 reduce-scatter.36
  772.8 9.2 reduce-scatter.26
  784.4 9.2 reduce-scatter.38
  795.9 10.4 reduce-scatter.42
  811.9 134.1 reduce-scatter.22
  948.2 8.2 reduce-scatter.46
  962.0 134.1 reduce-scatter.24
  1098.3 8.1 reduce-scatter.50
  1109.1 9.0 reduce-scatter.30
  1121.0 8.8 reduce-scatter.34
  1137.5 612.7 all-reduce.13
where the time goes:
time: 1780 us; the launch traced here: 1770 us
  waiting for transfers between devices  1320 us (74%)
  matrix products  172 us (10%)
  blocking collectives  112 us (6%)
  other arithmetic  109 us (6%)
  local copies, waits for them, and re-layouts  34.3 us (2%)
    psum x1, waiting for transfers between devices, body(): lax.psum((shares[0], shares[1], shares[2], shares[3], shares[4], shares[5...  562 us
    reduce_scatter x2, waiting for transfers between devices, layer_backward(): lax.psum_scatter(grad_values_all.reshape(seq_count, length, KV_HEADS * HE...  272 us
    reduce_scatter x2, waiting for transfers between devices, layer_backward(): lax.psum_scatter(grad_keys_all.reshape(seq_count, length, KV_HEADS * HEAD...  258 us
    all_gather x2, waiting for transfers between devices, layer_forward(): lax.all_gather(keys_own, 'ctx', axis=1, tiled=True)  109 us
    all_gather x2, waiting for transfers between devices, layer_forward(): lax.all_gather(values_own, 'ctx', axis=1, tiled=True)  55.6 us
    psum x1, blocking collectives, body(): lax.psum((shares[0], shares[1], shares[2], shares[3], shares[4], shares[5...  45.2 us
    convert_element_type x4, other arithmetic, attend_back(): grad_scores = (probabilities * (grad_probs - jnp.sum(probabilities * grad...  45 us
    all_gather x1, blocking collectives, body(): places = lax.all_gather(positions, 'ctx', axis=1, tiled=True)  42.7 us
  transfers between devices with their start and end apart: 29, of which 17 were waited for; matrix products, arithmetic and copies ran while one was open for 12% of the time, Pallas kernels for 0%

commit v1 on v0

--- a/solution.py
+++ b/solution.py
@@ -8,6 +8,25 @@
 HEAD = 64
 EPS = 1e-05
 ROPE_BASE = 100000.0
+
+
+def gather_around(shard, axis, dim):
+    size, place, span = (lax.axis_size(axis), lax.axis_index(axis), shard.shape[dim])
+    right = [(i, (i + 1) % size) for i in range(size)]
+    left = [(i, (i - 1) % size) for i in range(size)]
+    out = jnp.zeros((*shard.shape[:dim], size * span, *shard.shape[dim + 1 :]), shard.dtype)
+    out = lax.dynamic_update_slice_in_dim(out, shard, place * span, axis=dim)
+    from_left = from_right = shard
+    halfway = size // 2
+    for lap in range(1, halfway + 1):
+        from_left = lax.ppermute(from_left, axis, right)
+        out = lax.dynamic_update_slice_in_dim(out, from_left, (place - lap) % size * span, axis=dim)
+        if lap < size - halfway:
+            from_right = lax.ppermute(from_right, axis, left)
+            out = lax.dynamic_update_slice_in_dim(
+                out, from_right, (place + lap) % size * span, axis=dim
+            )
+    return out
 
 
 def rotate(tensor, positions_row, direction_sign):
@@ -109,7 +128,7 @@
     keys_own = keys_own.reshape(seq_count, row_count, KV_HEADS * HEAD)
     values_own = value_pre.astype(jnp.bfloat16)
     keys_all, values_all = (
-        lax.all_gather(keys_own, "ctx", axis=1, tiled=True),
+        gather_around(keys_own, "ctx", 1),
         lax.all_gather(values_own, "ctx", axis=1, tiled=True),
     )
     length = keys_all.shape[1]

time: 1780 us -> 1810 us (1.017)
  starting transfers between devices: 1.65 us -> 84.4 us
  waiting for transfers between devices: 1320 us -> 1270 us
    ppermute x0 -> x30, starting transfers between devices: none -> 82.8 us  [the longest x14 79.7 us: gather_around(): from_right = lax.ppermute(from_right, axis, left)]
    all_gather x2, waiting for transfers between devices: 55.6 us -> 0.04 us  [layer_forward(): lax.all_gather(values_own, 'ctx', axis=1, tiled=True)]
    ppermute x0 -> x30, waiting for transfers between devices: none -> 48.3 us  [the longest x16 46 us: gather_around(): from_left = lax.ppermute(from_left, axis, right)]
    all_gather x2, waiting for transfers between devices: 109 us -> 75.2 us  [layer_backward(): lax.all_gather(keys_own, 'ctx', axis=1, tiled=True)]
  transfers between devices with their start and end apart: 29 -> 59, of which waited for: 17 -> 31; matrix products, arithmetic and copies ran while one was open for 12% -> 12% of each run, Pallas kernels for 0% -> 0%
where the time goes in v1:
time: 1810 us; the launch traced here: 1800 us
  waiting for transfers between devices  1270 us (70%)
  matrix products  163 us (9%)
  other arithmetic  109 us (6%)
  blocking collectives  108 us (6%)
  starting transfers between devices  84.4 us (5%)
  local copies, waits for them, and re-layouts  48.3 us (3%)
    psum x1, waiting for transfers between devices, body(): lax.psum((shares[0], shares[1], shares[2], shares[3], shares[4], shares[5...  563 us
    reduce_scatter x2, waiting for transfers between devices, layer_backward(): lax.psum_scatter(grad_values_all.reshape(seq_count, length, KV_HEADS * HE...  272 us
    reduce_scatter x2, waiting for transfers between devices, layer_backward(): lax.psum_scatter(grad_keys_all.reshape(seq_count, length, KV_HEADS * HEAD...  257 us
    ppermute x14, starting transfers between devices, gather_around(): from_right = lax.ppermute(from_right, axis, left)  79.7 us
    all_gather x2, waiting for transfers between devices, layer_backward(): lax.all_gather(keys_own, 'ctx', axis=1, tiled=True)  75.2 us
    ppermute x16, waiting for transfers between devices, gather_around(): from_left = lax.ppermute(from_left, axis, right)  46 us
    psum x1, blocking collectives, body(): lax.psum((shares[0], shares[1], shares[2], shares[3], shares[4], shares[5...  45.1 us
    convert_element_type x4, other arithmetic, attend_back(): grad_scores = (probabilities * (grad_probs - jnp.sum(probabilities * grad...  44.3 us
  transfers between devices with their start and end apart: 59, of which 31 were waited for; matrix products, arithmetic and copies ran while one was open for 12% of the time, Pallas kernels for 0%

profile of v1, /device:TPU:0, one launch (start us, length us, event | category | flops | bytes accessed | tf_op | source)
XLA Modules:
  0.0 1800.6 jit_solution(4168971713860009152)
XLA Ops:
  39.8 38.4 %all_gather.92 = s32[2,2048]{1,0:T(2,128)S(1)} all-gather(s32[2,128]{1,0:T(2,128)} %param.21), channel_id=1, replica_groups=mesh['ctx'=16,'fsdp'=2] {'ctx'}, dimensions={1}, use_global_device_ids=true | all-gather | bytes 17408 | tf_op jit(solution)/shard_map/all_gather | solution.py:303
  108.5 5.7 collective-permute-start.7
  124.9 5.8 collective-permute-start.11
  133.1 5.9 collective-permute-start.13
  141.6 8.1 collective-permute-done.14
  149.8 14.5 while.52
  202.5 6.1 collective-permute-start.18
  211.2 5.9 collective-permute-start.20
  220.4 6.2 collective-permute-start.22
  228.8 6.1 collective-permute-start.24
  256.0 8.1 collective-permute-done.29
  264.2 15.9 while.53
  294.9 29.4 %all-gather.33.cloned.1.call-done = bf16[2,2048,192]{1,2,0:T(8,128)(2,1)} async-done(((bf16[2,128,192]{1,2,0:T(8,128)(2,1)}), bf16[2,2048,192]{1,2,0:T(8,128)(2,1)}) %all-gather.33.cloned.1.call-update) | async-done | bytes 1572880 | tf_op jit(solution)/shard_map/all_gather | solution.py:216
  329.3 63.6 %while.54 = (s32[]{:T(128)}, f32[2,128,3,3,64]{1,4,3,2,0:T(8,128)}, f32[2,2048,3,64]{1,3,2,0:T(8,128)}, f32[2,2048,3,64]{1,3,2,0:T(8,128)}, bf16[2,2048,3,64]{1,...) while((s32[]{:T(128)}, f32[2,128,3,3,64]{1,4,3,2,0:T(8,128)}, ...), condition=%wide.region_15.16_spmd, body=%wide.region_13.15_spmd.sunk | while | flops 1546066816 | bytes 160072944 | solution.py:220
  337.3 11.0 fusion.326
  369.0 11.0 fusion.326
  404.5 119.6 %reduce-scatter.19.cloned.1.call-done = f32[2,128,192]{1,2,0:T(8,128)} async-done(((f32[2,2048,192]{1,2,0:T(8,128)}), f32[2,128,192]{1,2,0:T(8,128)}) %reduce-scatter.19.cloned.1.call-update) | async-done | bytes 196624 | tf_op jit(solution)/shard_map/reduce_scatter | solution.py:233
  526.7 134.9 %reduce-scatter.21.cloned.1.call-done = f32[2,128,192]{1,2,0:T(8,128)} async-done(((f32[2,2048,192]{1,2,0:T(8,128)}), f32[2,128,192]{1,2,0:T(8,128)}) %reduce-scatter.21.cloned.1.call-update) | async-done | bytes 196624 | tf_op jit(solution)/shard_map/reduce_scatter | solution.py:239
  674.1 45.8 %all-gather.35.cloned.1.call-done = bf16[2,2048,192]{1,2,0:T(8,128)(2,1)} async-done(((bf16[2,128,192]{1,2,0:T(8,128)(2,1)}), bf16[2,2048,192]{1,2,0:T(8,128)(2,1)}) %all-gather.35.cloned.1.call-update) | async-done | bytes 1572880 | tf_op jit(solution)/shard_map/all_gather | solution.py:216
  724.9 65.2 %while.55 = (s32[]{:T(128)}, f32[2,128,3,3,64]{1,4,3,2,0:T(8,128)}, f32[2,2048,3,64]{1,3,2,0:T(8,128)}, f32[2,2048,3,64]{1,3,2,0:T(8,128)}, bf16[2,2048,3,64]{1,...) while((s32[]{:T(128)}, f32[2,128,3,3,64]{1,4,3,2,0:T(8,128)}, ...), condition=%wide.region_22.23_spmd, body=%wide.region_20.22_spmd.sunk | while | flops 1546066816 | bytes 160072944 | solution.py:220
  732.8 11.3 fusion.341
  748.2 5.9 fusion.343
  766.0 11.0 fusion.341
  826.1 10.8 reduce-scatter.43.cloned.1.call-done
  839.6 137.1 %reduce-scatter.23.cloned.1.call-done = f32[2,128,192]{1,2,0:T(8,128)} async-done(((f32[2,2048,192]{1,2,0:T(8,128)}), f32[2,128,192]{1,2,0:T(8,128)}) %reduce-scatter.23.cloned.1.call-update) | async-done | bytes 196624 | tf_op jit(solution)/shard_map/reduce_scatter | solution.py:233
  978.7 8.4 reduce-scatter.47.cloned.1.call-done
  989.7 137.1 %reduce-scatter.25.cloned.1.call-done = f32[2,128,192]{1,2,0:T(8,128)} async-done(((f32[2,2048,192]{1,2,0:T(8,128)}), f32[2,128,192]{1,2,0:T(8,128)}) %reduce-scatter.25.cloned.1.call-update) | async-done | bytes 196624 | tf_op jit(solution)/shard_map/reduce_scatter | solution.py:239
  1128.8 8.3 reduce-scatter.51.cloned.1.call-done
  1139.6 9.2 reduce-scatter.31.cloned.1.call-done
  1150.6 10.0 reduce-scatter.35.cloned.1.call-done
  1170.8 45.1 %all-reduce.8 = (f32[1,288]{1,0:T(1,128)S(1)}, f32[1,288]{1,0:T(1,128)S(1)}, f32[1,288]{1,0:T(1,128)S(1)}, f32[1,288]{1,0:T(1,128)S(1)}) all-reduce(f32[1,288]{1,0:T(1,128)S(1)} %stack.82, f32[1,288]{1,0:T(1,128)S(1)} %stack.81, f32[1,288]{1,0:T(1,128)S(1)} %stack.97, ...), channel_id=1, replica_groups=mesh['ctx'=16,'fsdp'=2] {'ctx'}, use_global_device_ids=true, to_apply=%region_31.32 | all-reduce | flops 1152 | bytes 9216 | tf_op jit(solution)/shard_map/psum | solution.py:369
  1218.1 562.8 %all-reduce.14.cloned.1.call-done = (f32[1,288,576]{2,1,0:T(8,128)}, f32[1,288,576]{2,1,0:T(8,128)}, f32[1,288,192]{2,1,0:T(8,128)}, f32[1,288,192]{2,1,0:T(8,12...) async-done(((f32[1,288,576]{2,1,0:T(8,128)}, ...) | async-done | bytes 14155792 | tf_op jit(solution)/shard_map/psum | solution.py:369
  (629 shorter events, 377.0 us)
Async XLA Ops:
  7.2 142.6 %all-gather.29.cloned.1.call-start = ((), (), s32[]{:S(2)}) async-start(), calls=%async_computation.18 | async-start | bytes 1671168 | tf_op jit(solution)/shard_map/all_gather | solution.py:132
  18.9 146.8 %all-gather.37.cloned.1.call-start = ((), (), s32[]{:S(2)}) async-start(), calls=%async_computation.40 | async-start | bytes 2654208 | tf_op jit(solution)/shard_map/all_gather | solution.py:315
  21.9 147.4 %all-gather.39.cloned.1.call-start = ((), (), s32[]{:S(2)}) async-start(), calls=%async_computation.41 | async-start | bytes 2654208 | tf_op jit(solution)/shard_map/all_gather | solution.py:316
  23.3 150.0 %all-gather.41.cloned.1.call-start = ((), (), s32[]{:S(2)}) async-start(), calls=%async_computation.42 | async-start | bytes 2654208 | tf_op jit(solution)/shard_map/all_gather | solution.py:317
  26.2 161.2 %all-gather.47.cloned.1.call-start = ((), (), s32[]{:S(2)}) async-start(), calls=%async_computation.45 | async-start | bytes 2654208 | tf_op jit(solution)/shard_map/all_gather | solution.py:317
  32.8 58.6 %collective-permute-start = (bf16[2,128,192]{1,2,0:T(8,128)(2,1)}, bf16[2,128,192]{1,2,0:T(8,128)(2,1)}, u32[]{:S(2)}, u32[]{:S(2)}) collective-permute-start(bf16[2,128,192]{1,2,0:T(8,128)(2,1)} %bitcast.81), channel_id=1, source_target_pairs={{0,2},{2,4},{4,6},{6,8},{8,10},{10,12},{12,14},{14,16},{16,18},{18... | collective-permute-start | bytes 294920 | tf_op jit(solution)/shard_map/ppermute | solution.py:22
  35.6 55.9 %collective-permute-start.1 = (bf16[2,128,192]{1,2,0:T(8,128)(2,1)}, bf16[2,128,192]{1,2,0:T(8,128)(2,1)}, u32[]{:S(2)}, u32[]{:S(2)}) collective-permute-start(bf16[2,128,192]{1,2,0:T(8,128)(2,1)} %bitcast.81), channel_id=1, source_target_pairs={{0,30},{2,0},{4,2},{6,4},{8,6},{10,8},{12,10},{14,12},{16,14},{18,... | collective-permute-start | bytes 294920 | tf_op jit(solution)/shard_map/ppermute | solution.py:25
  39.7 224.6 %all-gather.31.cloned.1.call-start = ((), (), s32[]{:S(2)}) async-start(), calls=%async_computation.19 | async-start | bytes 1671168 | tf_op jit(solution)/shard_map/all_gather | solution.py:132
  177.3 104.5 %all-gather.45.cloned.1.call-start = ((), (), s32[]{:S(2)}) async-start(), calls=%async_computation.44 | async-start | bytes 2654208 | tf_op jit(solution)/shard_map/all_gather | solution.py:316
  178.1 107.3 %all-gather.43.cloned.1.call-start = ((), (), s32[]{:S(2)}) async-start(), calls=%async_computation.43 | async-start | bytes 2654208 | tf_op jit(solution)/shard_map/all_gather | solution.py:315
  178.9 145.5 %all-gather.33.cloned.1.call-start = ((), (), s32[]{:S(2)}) async-start(), calls=%async_computation.20 | async-start | bytes 1671168 | tf_op jit(solution)/shard_map/all_gather | solution.py:216
  191.7 10.8 collective-permute-start.16
  197.9 326.2 %reduce-scatter.19.cloned.1.call-start = ((), (), s32[]{:S(2)}) async-start(), calls=%async_computation.21 | async-start | bytes 3342336 | tf_op jit(solution)/shard_map/reduce_scatter | solution.py:233
  393.0 268.6 %reduce-scatter.21.cloned.1.call-start = ((), (), s32[]{:S(2)}) async-start(), calls=%async_computation.22 | async-start | bytes 3342336 | tf_op jit(solution)/shard_map/reduce_scatter | solution.py:239
  393.7 326.2 %all-gather.35.cloned.1.call-start = ((), (), s32[]{:S(2)}) async-start(), calls=%async_computation.23 | async-start | bytes 1671168 | tf_op jit(solution)/shard_map/all_gather | solution.py:216
  394.3 407.7 %reduce-scatter.29.cloned.1.call-start = ((), (), s32[]{:S(2)}) async-start(), calls=%async_computation.27 | async-start | bytes 1105920 | tf_op jit(solution)/shard_map/reduce_scatter | solution.py:344
  395.9 410.0 %reduce-scatter.41.cloned.1.call-start = ((), (), s32[]{:S(2)}) async-start(), calls=%async_computation.33 | async-start | bytes 1105920 | tf_op jit(solution)/shard_map/reduce_scatter | solution.py:353
  397.4 410.4 %reduce-scatter.53.cloned.1.call-start = ((), (), s32[]{:S(2)}) async-start(), calls=%async_computation.39 | async-start | bytes 2654208 | tf_op jit(solution)/shard_map/reduce_scatter | solution.py:365
  399.3 411.0 %reduce-scatter.45.cloned.1.call-start = ((), (), s32[]{:S(2)}) async-start(), calls=%async_computation.35 | async-start | bytes 2654208 | tf_op jit(solution)/shard_map/reduce_scatter | solution.py:359
  402.4 410.4 %reduce-scatter.49.cloned.1.call-start = ((), (), s32[]{:S(2)}) async-start(), calls=%async_computation.37 | async-start | bytes 2654208 | tf_op jit(solution)/shard_map/reduce_scatter | solution.py:362
  404.5 411.0 %reduce-scatter.33.cloned.1.call-start = ((), (), s32[]{:S(2)}) async-start(), calls=%async_computation.29 | async-start | bytes 442368 | tf_op jit(solution)/shard_map/reduce_scatter | solution.py:347
  673.9 143.3 %reduce-scatter.37.cloned.1.call-start = ((), (), s32[]{:S(2)}) async-start(), calls=%async_computation.31 | async-start | bytes 442368 | tf_op jit(solution)/shard_map/reduce_scatter | solution.py:350
  792.1 26.7 %reduce-scatter.27.cloned.1.call-start = ((), (), s32[]{:S(2)}) async-start(), calls=%async_computation.26 | async-start | bytes 1105920 | tf_op jit(solution)/shard_map/reduce_scatter | solution.py:344
  794.7 29.5 %reduce-scatter.39.cloned.1.call-start = ((), (), s32[]{:S(2)}) async-start(), calls=%async_computation.32 | async-start | bytes 1105920 | tf_op jit(solution)/shard_map/reduce_scatter | solution.py:353
  796.1 40.8 %reduce-scatter.43.cloned.1.call-start = ((), (), s32[]{:S(2)}) async-start(), calls=%async_computation.34 | async-start | bytes 2654208 | tf_op jit(solution)/shard_map/reduce_scatter | solution.py:359
  798.1 178.5 %reduce-scatter.23.cloned.1.call-start = ((), (), s32[]{:S(2)}) async-start(), calls=%async_computation.24 | async-start | bytes 3342336 | tf_op jit(solution)/shard_map/reduce_scatter | solution.py:233
  798.8 188.3 %reduce-scatter.47.cloned.1.call-start = ((), (), s32[]{:S(2)}) async-start(), calls=%async_computation.36 | async-start | bytes 2654208 | tf_op jit(solution)/shard_map/reduce_scatter | solution.py:362
  801.2 325.6 %reduce-scatter.25.cloned.1.call-start = ((), (), s32[]{:S(2)}) async-start(), calls=%async_computation.25 | async-start | bytes 3342336 | tf_op jit(solution)/shard_map/reduce_scatter | solution.py:239
  801.9 335.2 %reduce-scatter.51.cloned.1.call-start = ((), (), s32[]{:S(2)}) async-start(), calls=%async_computation.38 | async-start | bytes 2654208 | tf_op jit(solution)/shard_map/reduce_scatter | solution.py:365
  805.8 343.1 %reduce-scatter.31.cloned.1.call-start = ((), (), s32[]{:S(2)}) async-start(), calls=%async_computation.28 | async-start | bytes 442368 | tf_op jit(solution)/shard_map/reduce_scatter | solution.py:347
  978.7 181.9 %reduce-scatter.35.cloned.1.call-start = ((), (), s32[]{:S(2)}) async-start(), calls=%async_computation.30 | async-start | bytes 442368 | tf_op jit(solution)/shard_map/reduce_scatter | solution.py:350
  1128.8 652.1 %all-reduce.14.cloned.1.call-start = ((), (), s32[]{:S(2)}) async-start(), calls=%async_computation.46 | async-start | bytes 29491200 | tf_op jit(solution)/shard_map/psum | solution.py:369
  (154 other events, 2378.0 us)
Sparse Core Ops, SparseCore 0:
  19.0 59.4 all-gather.28
  80.6 8.2 all-gather.36
  91.1 11.2 all-gather.38
  103.7 11.2 all-gather.40
  117.0 11.2 all-gather.46
  177.5 60.9 all-gather.30
  240.6 9.0 all-gather.44
  251.7 11.2 all-gather.42
  266.3 57.9 all-gather.32
  393.1 130.9 reduce-scatter.18
  529.6 131.8 reduce-scatter.20
  664.1 55.7 all-gather.34
  722.2 6.2 reduce-scatter.28
  730.7 9.1 reduce-scatter.40
  742.0 10.3 reduce-scatter.52
  755.1 10.5 reduce-scatter.44
  767.8 10.5 reduce-scatter.48
  781.1 9.0 reduce-scatter.32
  792.4 8.8 reduce-scatter.36
  803.4 9.1 reduce-scatter.26
  814.9 9.2 reduce-scatter.38
  826.5 10.4 reduce-scatter.42
  842.5 134.0 reduce-scatter.22
  978.8 8.3 reduce-scatter.46
  992.7 134.0 reduce-scatter.24
  1128.9 8.1 reduce-scatter.50
  1139.8 9.0 reduce-scatter.30
  1151.7 8.8 reduce-scatter.34
  1168.2 612.6 all-reduce.13
